TPU v7x, 32 devices: a whole 2x2x4 slice. The times are simulated.
32 devices in a mesh: vocab: 4 (over y, x), dp: 8 (over z, core).
Axes of the slice: x: 2, y: 2, z: 4, core: 2. Of those that a mesh axis runs over, the one named last changes fastest.
Arguments:
- grads: bfloat16 [4096, 4096], P(('vocab', 'dp')), may hold values from -6 to 6
- token_ids: int32 [4096], P(('vocab', 'dp')), may hold values from 0 to 32063, as said below
Outputs:
- grad_table: float32 [32064, 4096], P('vocab', 'dp')
- row_share: float32 [32064], P('vocab')
Inputs may be any that keep to these rules, and one draw needn't show every extreme that they name: `token_ids`: within the 128 ids of one device (aligned blocks in order) the ids never fall; at most 32 of them lie in the rows k * 8016 to (k + 1) * 8016 - 1 of any one k, and in every block some k has exactly 32.
All inputs are finite; a program needn't handle non-finite values.
Results may differ from a plain program's by a relative error of at most 0.0003.
Values may be sent and summed in bfloat16 or wider, within the bound.
No kernel may reach another device: no remote copies, remote signals or barrier semaphores. Data moves between devices by JAX's collectives and lax.ppermute only.
A program may use at most 64 MiB of HBM per device.

v0:
```python
import math
import jax
import jax.numpy as jnp
from jax import lax
from jax.sharding import PartitionSpec as P

VOCAB_DEV = 8016
TOK_DEV = 128
CAP = 32


def bucket(id_blocks, data_blocks, n_vocab):
    owner_start = jnp.arange(n_vocab, dtype=jnp.int32) * VOCAB_DEV
    starts = jnp.sum((id_blocks[:, None, :] < owner_start[None, :, None]).astype(jnp.int32), axis=2)
    length = id_blocks.shape[1]
    finish = jnp.concatenate(
        [starts[:, 1:], jnp.full((starts.shape[0], 1), length, jnp.int32)], axis=1
    )
    amount = jnp.transpose(finish - starts, (1, 0))
    begins = jnp.transpose(starts, (1, 0))
    slot = jnp.arange(CAP, dtype=jnp.int32)
    places = begins[:, :, None] + slot[None, None, :]
    valid = slot[None, None, :] < amount[:, :, None]
    columns = jnp.arange(length, dtype=jnp.int32)
    select = (places[:, :, :, None] == columns[None, None, None, :]) & valid[:, :, :, None]
    rows = jnp.einsum(
        "vbcl,bld->vbcd",
        select.astype(data_blocks.dtype),
        data_blocks,
        preferred_element_type=jnp.float32,
    )
    rows = rows.astype(data_blocks.dtype).reshape(-1, data_blocks.shape[2])
    picked = jnp.sum(jnp.where(select, id_blocks[None, :, None, :], 0), axis=3)
    slot_ids = jnp.where(valid, picked, -1).reshape(-1)
    return (rows, slot_ids)


def local(grads, token_ids):
    n_vocab = lax.axis_size("vocab")
    n_data = lax.axis_size("dp")
    spread_ids = jnp.broadcast_to(token_ids[:, None], (token_ids.shape[0], n_data))
    split_rows, split_ids = (
        lax.all_to_all(grads, "dp", split_axis=1, concat_axis=0, tiled=True),
        lax.all_to_all(spread_ids, "dp", split_axis=1, concat_axis=0, tiled=True),
    )
    group_ids = split_ids.reshape(n_data, -1)
    group_rows = split_rows.reshape(n_data, group_ids.shape[1], split_rows.shape[1])
    rows, slot_ids = bucket(group_ids, group_rows, n_vocab)
    mine, mine_ids = (
        lax.all_to_all(rows, "vocab", split_axis=0, concat_axis=0, tiled=True),
        lax.all_to_all(slot_ids, "vocab", split_axis=0, concat_axis=0, tiled=True),
    )
    local_rows = jnp.where(mine_ids < 0, -1, mine_ids - lax.axis_index("vocab") * VOCAB_DEV)
    total = local_rows.shape[0]
    width = math.gcd(total, 512)
    row_blocks = mine.reshape(total // width, width, mine.shape[1])
    id_parts = local_rows.reshape(total // width, width)
    table_rows = jnp.arange(VOCAB_DEV, dtype=jnp.int32)

    def accumulate(carry, item):
        table, counts = carry
        block, ids = item
        onehot = ids[:, None] == table_rows[None, :]
        table = table + lax.dot_general(
            onehot.astype(block.dtype),
            block,
            (((0,), (0,)), ((), ())),
            preferred_element_type=jnp.float32,
        )
        counts = counts + jnp.sum(onehot.astype(jnp.float32), axis=0)
        return ((table, counts), None)

    start = (
        jnp.zeros((VOCAB_DEV, mine.shape[1]), jnp.float32),
        jnp.zeros((VOCAB_DEV,), jnp.float32),
    )
    (grad_table, counts), _ = lax.scan(accumulate, start, (row_blocks, id_parts))
    row_share = counts * (VOCAB_DEV / (TOK_DEV * n_data))
    return (grad_table, row_share)


def solution(mesh):
    in_specs = (P(("vocab", "dp"), None), P(("vocab", "dp")))
    out_specs = (P("vocab", "dp"), P("vocab"))
    return jax.shard_map(local, mesh=mesh, in_specs=in_specs, out_specs=out_specs, check_vma=False)
```

profile of v0, /device:TPU:0, one launch (start us, length us, event | category | flops | bytes accessed | tf_op | source)
XLA Modules:
  0.0 92.9 jit_solution(14292049239312270715)
XLA Ops:
  0.6 1.3 %broadcast_in_dim.26 = s32[128,8,1]{0,2,1:T(1,128)} broadcast(s32[128]{0:T(128)} %param.5), dimensions={0} | broadcast | bytes 4608 | tf_op jit(solution)/shard_map/broadcast_in_dim | solution.py:41
  1.9 6.4 %all-to-all-start = ((s32[128,8,1]{0,2,1:T(1,128)}), s32[128,8,1]{0,2,1:T(1,128)S(1)}, u32[]{:S(2)}, u32[]{:S(2)}) async-start(s32[128,8,1]{0,2,1:T(1,128)} %broadcast_in_dim.26), calls=%async_computation | async-start | bytes 8192 | tf_op jit(solution)/shard_map/all_to_all | solution.py:44
  8.2 1.6 %copy.29 = bf16[128,4096]{0,1:T(8,128)(2,1)S(1)} copy(bf16[128,4096]{1,0:T(8,128)(2,1)} %param.4) | data formatting | bytes 2097152 | tf_op args[0]
  9.9 1.3 %copy.30 = bf16[128,8,512]{2,0,1:T(8,128)(2,1)} copy(bf16[128,8,512]{0,2,1:T(8,128)(2,1)S(1)} %bitcast.29) | data formatting | bytes 2097152 | tf_op jit(solution)/shard_map/all_to_all | solution.py:43
  11.2 2.6 %all-to-all-done = s32[128,8,1]{0,2,1:T(1,128)S(1)} async-done(((s32[128,8,1]{0,2,1:T(1,128)}), s32[128,8,1]{0,2,1:T(1,128)S(1)}, u32[]{:S(2)}, u32[]{:S(2)}) %all-to-all-start) | async-done | bytes 4128 | tf_op jit(solution)/shard_map/all_to_all | solution.py:44
  13.7 3.6 %all-to-all-start.2 = ((bf16[128,8,512]{2,0,1:T(8,128)(2,1)}), bf16[128,8,512]{2,0,1:T(8,128)(2,1)S(1)}, u32[]{:S(2)}, u32[]{:S(2)}) async-start(bf16[128,8,512]{2,0,1:T(8,128)(2,1)} %copy.30), calls=%async_computation.2 | async-start | bytes 2097152 | tf_op jit(solution)/shard_map/all_to_all | solution.py:43
  17.3 0.1 add.37
  17.4 0.2 convert_reduce_fusion
  17.6 0.1 iota_compare_fusion.5
  17.7 0.1 copy.23
  17.8 0.1 iota_add_fusion
  17.9 0.9 select_reduce_fusion
  18.8 0.1 reduce_sum.31
  18.9 0.1 lt.57
  19.0 0.1 lt.58
  19.1 0.6 copy.26
  19.7 24.1 %all-to-all-done.2 = bf16[128,8,512]{2,0,1:T(8,128)(2,1)S(1)} async-done(((bf16[128,8,512]{2,0,1:T(8,128)(2,1)}), bf16[128,8,512]{2,0,1:T(8,128)(2,1)S(1)}, u32[]{:S(2)}, u32[]{:S(2)}) %all-to-all-start.2) | async-done | bytes 1048608 | tf_op jit(solution)/shard_map/all_to_all | solution.py:43
  43.8 3.7 %all-to-all-start.1 = ((s32[4,256,1]{1,2,0:T(1,128)}), s32[4,256,1]{1,2,0:T(1,128)S(1)}, u32[]{:S(2)}, u32[]{:S(2)}) async-start(s32[4,256,1]{1,2,0:T(1,128)} %copy.26), calls=%async_computation.1 | async-start | bytes 8192 | tf_op jit(solution)/shard_map/all_to_all | solution.py:51
  47.5 0.5 fusion.9
  48.0 1.1 %copy.31 = bf16[4,8,32,512]{3,2,1,0:T(8,128)(2,1)} copy(bf16[4,8,32,512]{3,2,0,1:T(8,128)(2,1)S(1)} %fusion.9) | data formatting | bytes 2097152 | tf_op jit(solution)/shard_map/convert_element_type | solution.py:32
  49.1 3.1 %all-to-all-done.1 = s32[4,256,1]{1,2,0:T(1,128)S(1)} async-done(((s32[4,256,1]{1,2,0:T(1,128)}), s32[4,256,1]{1,2,0:T(1,128)S(1)}, u32[]{:S(2)}, u32[]{:S(2)}) %all-to-all-start.1) | async-done | bytes 4128 | tf_op jit(solution)/shard_map/all_to_all | solution.py:51
  52.2 3.5 %all-to-all-start.3 = ((bf16[4,256,512]{2,1,0:T(8,128)(2,1)}), bf16[4,256,512]{2,1,0:T(8,128)(2,1)S(1)}, u32[]{:S(2)}, u32[]{:S(2)}) async-start(bf16[4,256,512]{2,1,0:T(8,128)(2,1)} %bitcast.10), calls=%async_computation.3 | async-start | bytes 2097152 | tf_op jit(solution)/shard_map/all_to_all | solution.py:50
  55.8 12.1 %all-to-all-done.3 = bf16[4,256,512]{2,1,0:T(8,128)(2,1)S(1)} async-done(((bf16[4,256,512]{2,1,0:T(8,128)(2,1)}), bf16[4,256,512]{2,1,0:T(8,128)(2,1)S(1)}, u32[]{:S(2)}, u32[]{:S(2)}) %all-to-all-start.3) | async-done | bytes 1048608 | tf_op jit(solution)/shard_map/all_to_all | solution.py:50
  67.9 24.4 %while.13 = (s32[]{:T(128)}, f32[8016,512]{1,0:T(8,128)}, f32[8016]{0:T(1024)S(1)}, s32[2,512]{1,0:T(2,128)S(1)}, bf16[2,512,512]{2,1,0:T(8,128)(2,1)S(1)}, /*index=5*/s32[]{:T(128)}, s32[]{:T(128)}) while((s32[]{:T(128)}, f32[8016,512]{1,0:T(8,128)}, f32[8016]{0:T(1024)S(1)}, s32[2,512]{1,0:T(2,128)S(1)}, ...), condition=%wide.region_4.5_spmd.clone, body=%wide.region_2.4_spmd.clone.sunk | while | flops 4227325952 | bytes 33494372 | solution.py:77
  67.9 1.8 %fusion.18 = f32[8016]{0:T(1024)S(1)} fusion(s32[512]{0:T(512)S(1)} %bitcast.30), kind=kLoop, calls=%fused_computation.4.clone.1 | loop fusion | flops 12304560 | bytes 34112 | tf_op jit(solution)/shard_map/while/body/eval_jaxpr/reduce_sum | solution.py:70
  69.7 8.7 %select_add_fusion.4 = f32[8016,512]{1,0:T(8,128)} fusion(f32[8016,512]{1,0:T(8,128)} %get-tuple-element.106, s32[512]{0:T(512)S(1)} %bitcast.31, pred[]{:T(512)S(6)} %compare.4, bf16[2,512,512]{2,1,0:T(8,128)(2,1)S(1)} %get-tuple-element.116, s32[]{:T(128)S(6)} %copy.37), kind=kOutput, calls=%fused_computation.5.clone.1 | convolution fusion | flops 4215005184 | bytes 33359876 | tf_op jit(solution)/shard_map/while/body/eval_jaxpr/dot_general | solution.py:64
  78.4 1.8 %fusion.18 = f32[8016]{0:T(1024)S(1)} fusion(s32[512]{0:T(512)S(1)} %bitcast.30), kind=kLoop, calls=%fused_computation.4.clone.1 | loop fusion | flops 12304560 | bytes 34112 | tf_op jit(solution)/shard_map/while/body/eval_jaxpr/reduce_sum | solution.py:70
  80.3 12.0 %select_add_fusion.4 = f32[8016,512]{1,0:T(8,128)} fusion(f32[8016,512]{1,0:T(8,128)} %get-tuple-element.106, s32[512]{0:T(512)S(1)} %bitcast.31, pred[]{:T(512)S(6)} %compare.4, bf16[2,512,512]{2,1,0:T(8,128)(2,1)S(1)} %get-tuple-element.116, s32[]{:T(128)S(6)} %copy.37), kind=kOutput, calls=%fused_computation.5.clone.1 | convolution fusion | flops 4215005184 | bytes 33359876 | tf_op jit(solution)/shard_map/while/body/eval_jaxpr/dot_general | solution.py:64
  92.3 0.6 broadcast_multiply_fusion
  (15 shorter events, 0.1 us)
Async XLA Ops:
  1.9 11.9 %all-to-all-start = ((s32[128,8,1]{0,2,1:T(1,128)}), s32[128,8,1]{0,2,1:T(1,128)S(1)}, u32[]{:S(2)}, u32[]{:S(2)}) async-start(s32[128,8,1]{0,2,1:T(1,128)} %broadcast_in_dim.26), calls=%async_computation | async-start | bytes 8192 | tf_op jit(solution)/shard_map/all_to_all | solution.py:44
  13.7 30.1 %all-to-all-start.2 = ((bf16[128,8,512]{2,0,1:T(8,128)(2,1)}), bf16[128,8,512]{2,0,1:T(8,128)(2,1)S(1)}, u32[]{:S(2)}, u32[]{:S(2)}) async-start(bf16[128,8,512]{2,0,1:T(8,128)(2,1)} %copy.30), calls=%async_computation.2 | async-start | bytes 2097152 | tf_op jit(solution)/shard_map/all_to_all | solution.py:43
  43.8 8.4 %all-to-all-start.1 = ((s32[4,256,1]{1,2,0:T(1,128)}), s32[4,256,1]{1,2,0:T(1,128)S(1)}, u32[]{:S(2)}, u32[]{:S(2)}) async-start(s32[4,256,1]{1,2,0:T(1,128)} %copy.26), calls=%async_computation.1 | async-start | bytes 8192 | tf_op jit(solution)/shard_map/all_to_all | solution.py:51
  52.2 15.7 %all-to-all-start.3 = ((bf16[4,256,512]{2,1,0:T(8,128)(2,1)}), bf16[4,256,512]{2,1,0:T(8,128)(2,1)S(1)}, u32[]{:S(2)}, u32[]{:S(2)}) async-start(bf16[4,256,512]{2,1,0:T(8,128)(2,1)} %bitcast.10), calls=%async_computation.3 | async-start | bytes 2097152 | tf_op jit(solution)/shard_map/all_to_all | solution.py:50
where the time goes:
time: 93.3 us; the launch traced here: 92.9 us
  waiting for transfers between devices  41.9 us (45%)
  matrix products  21.2 us (23%)
  starting transfers between devices  17.1 us (18%)
  local copies, waits for them, and re-layouts  6.29 us (7%)
  other arithmetic  5.63 us (6%)
    all_to_all x1, waiting for transfers between devices, local(): lax.all_to_all(grads, 'dp', split_axis=1, concat_axis=0, tiled=True)  24.1 us
    dot_general x2, matrix products, accumulate(): lax.dot_general(onehot.astype(block.dtype), block, (((0,), (0,)), ((), ()...  20.7 us
    all_to_all x1, waiting for transfers between devices, local(): lax.all_to_all(rows, 'vocab', split_axis=0, concat_axis=0, tiled=True)  12.1 us
    all_to_all x1, starting transfers between devices, local(): lax.all_to_all(spread_ids, 'dp', split_axis=1, concat_axis=0, tiled=True)  6.35 us
    all_to_all x1, starting transfers between devices, local(): lax.all_to_all(slot_ids, 'vocab', split_axis=0, concat_axis=0, tiled=True)  3.72 us
    reduce_sum x2, other arithmetic, accumulate(): counts = counts + jnp.sum(onehot.astype(jnp.float32), axis=0)  3.68 us
    all_to_all x1, starting transfers between devices, local(): lax.all_to_all(grads, 'dp', split_axis=1, concat_axis=0, tiled=True)  3.56 us
    all_to_all x1, starting transfers between devices, local(): lax.all_to_all(rows, 'vocab', split_axis=0, concat_axis=0, tiled=True)  3.52 us
  transfers between devices with their start and end apart: 4, of which 4 were waited for; matrix products, arithmetic and copies ran while one was open for 7% of the time, Pallas kernels for 0%

commit v1 on v0

--- a/solution.py
+++ b/solution.py
@@ -41,7 +41,12 @@
     spread_ids = jnp.broadcast_to(token_ids[:, None], (token_ids.shape[0], n_data))
     split_rows, split_ids = (
         lax.all_to_all(grads, "dp", split_axis=1, concat_axis=0, tiled=True),
-        lax.all_to_all(spread_ids, "dp", split_axis=1, concat_axis=0, tiled=True),
+        jnp.concatenate(
+            lax.all_to_all(
+                jnp.stack(jnp.split(spread_ids, lax.axis_size("dp"), axis=1)), "dp", 0, 0
+            ),
+            axis=0,
+        ),
     )
     group_ids = split_ids.reshape(n_data, -1)
     group_rows = split_rows.reshape(n_data, group_ids.shape[1], split_rows.shape[1])

time: 93.3 us -> 93.3 us (level)
    another operation x0 -> x1, local copies, waits for them, and re-layouts: none -> 1.25 us  [local(): jnp.stack(jnp.split(spread_ids, lax.axis_size('dp'), axis=1))]
    broadcast_in_dim x1 -> x0, local copies, waits for them, and re-layouts: 1.25 us -> none  [local(): jnp.broadcast_to(token_ids[:, None], (token_ids.shape[0], n_data))]
where the time goes in v1:
time: 93.3 us; the launch traced here: 92.9 us
  waiting for transfers between devices  41.9 us (45%)
  matrix products  21.2 us (23%)
  starting transfers between devices  17.1 us (18%)
  local copies, waits for them, and re-layouts  6.29 us (7%)
  other arithmetic  5.63 us (6%)
    all_to_all x1, waiting for transfers between devices, local(): lax.all_to_all(grads, 'dp', split_axis=1, concat_axis=0, tiled=True)  24.1 us
    dot_general x2, matrix products, accumulate(): lax.dot_general(onehot.astype(block.dtype), block, (((0,), (0,)), ((), ()...  20.7 us
    all_to_all x1, waiting for transfers between devices, local(): lax.all_to_all(rows, 'vocab', split_axis=0, concat_axis=0, tiled=True)  12.1 us
    all_to_all x1, starting transfers between devices, local(): lax.all_to_all(jnp.stack(jnp.split(spread_ids, lax.axis_size('dp'), axis=...  6.35 us
    all_to_all x1, starting transfers between devices, local(): lax.all_to_all(slot_ids, 'vocab', split_axis=0, concat_axis=0, tiled=True)  3.72 us
    reduce_sum x2, other arithmetic, accumulate(): counts = counts + jnp.sum(onehot.astype(jnp.float32), axis=0)  3.68 us
    all_to_all x1, starting transfers between devices, local(): lax.all_to_all(grads, 'dp', split_axis=1, concat_axis=0, tiled=True)  3.56 us
    all_to_all x1, starting transfers between devices, local(): lax.all_to_all(rows, 'vocab', split_axis=0, concat_axis=0, tiled=True)  3.52 us
  transfers between devices with their start and end apart: 4, of which 4 were waited for; matrix products, arithmetic and copies ran while one was open for 7% of the time, Pallas kernels for 0%

profile of v1, /device:TPU:0, one launch (start us, length us, event | category | flops | bytes accessed | tf_op | source)
XLA Modules:
  0.0 92.9 jit_solution(14292049239312270715)
XLA Ops:
  0.6 1.3 %stack.2 = s32[8,128,1]{1,2,0:T(1,128)} broadcast(s32[128]{0:T(128)} %param.5), dimensions={1} | broadcast | bytes 4608 | tf_op jit(solution)/shard_map/stack | solution.py:46
  1.9 6.4 %all-to-all-start = ((s32[8,128,1]{1,2,0:T(1,128)}), s32[8,128,1]{1,2,0:T(1,128)S(1)}, u32[]{:S(2)}, u32[]{:S(2)}) async-start(s32[8,128,1]{1,2,0:T(1,128)} %stack.2), calls=%async_computation | async-start | bytes 8192 | tf_op jit(solution)/shard_map/all_to_all | solution.py:45
  8.2 1.6 %copy.29 = bf16[128,4096]{0,1:T(8,128)(2,1)S(1)} copy(bf16[128,4096]{1,0:T(8,128)(2,1)} %param.4) | data formatting | bytes 2097152 | tf_op args[0]
  9.9 1.3 %copy.30 = bf16[128,8,512]{2,0,1:T(8,128)(2,1)} copy(bf16[128,8,512]{0,2,1:T(8,128)(2,1)S(1)} %bitcast.27) | data formatting | bytes 2097152 | tf_op jit(solution)/shard_map/all_to_all | solution.py:43
  11.2 2.6 %all-to-all-done = s32[8,128,1]{1,2,0:T(1,128)S(1)} async-done(((s32[8,128,1]{1,2,0:T(1,128)}), s32[8,128,1]{1,2,0:T(1,128)S(1)}, u32[]{:S(2)}, u32[]{:S(2)}) %all-to-all-start) | async-done | bytes 4128 | tf_op jit(solution)/shard_map/all_to_all | solution.py:45
  13.7 3.6 %all-to-all-start.2 = ((bf16[128,8,512]{2,0,1:T(8,128)(2,1)}), bf16[128,8,512]{2,0,1:T(8,128)(2,1)S(1)}, u32[]{:S(2)}, u32[]{:S(2)}) async-start(bf16[128,8,512]{2,0,1:T(8,128)(2,1)} %copy.30), calls=%async_computation.2 | async-start | bytes 2097152 | tf_op jit(solution)/shard_map/all_to_all | solution.py:43
  17.3 0.1 add.37
  17.4 0.2 convert_reduce_fusion
  17.6 0.1 iota_compare_fusion.5
  17.7 0.1 copy.23
  17.8 0.1 iota_add_fusion
  17.9 0.9 select_reduce_fusion
  18.8 0.1 reduce_sum.31
  18.9 0.1 lt.57
  19.0 0.1 lt.58
  19.1 0.6 copy.26
  19.7 24.1 %all-to-all-done.2 = bf16[128,8,512]{2,0,1:T(8,128)(2,1)S(1)} async-done(((bf16[128,8,512]{2,0,1:T(8,128)(2,1)}), bf16[128,8,512]{2,0,1:T(8,128)(2,1)S(1)}, u32[]{:S(2)}, u32[]{:S(2)}) %all-to-all-start.2) | async-done | bytes 1048608 | tf_op jit(solution)/shard_map/all_to_all | solution.py:43
  43.8 3.7 %all-to-all-start.1 = ((s32[4,256,1]{1,2,0:T(1,128)}), s32[4,256,1]{1,2,0:T(1,128)S(1)}, u32[]{:S(2)}, u32[]{:S(2)}) async-start(s32[4,256,1]{1,2,0:T(1,128)} %copy.26), calls=%async_computation.1 | async-start | bytes 8192 | tf_op jit(solution)/shard_map/all_to_all | solution.py:56
  47.5 0.5 fusion.9
  48.0 1.1 %copy.31 = bf16[4,8,32,512]{3,2,1,0:T(8,128)(2,1)} copy(bf16[4,8,32,512]{3,2,0,1:T(8,128)(2,1)S(1)} %fusion.9) | data formatting | bytes 2097152 | tf_op jit(solution)/shard_map/convert_element_type | solution.py:32
  49.1 3.1 %all-to-all-done.1 = s32[4,256,1]{1,2,0:T(1,128)S(1)} async-done(((s32[4,256,1]{1,2,0:T(1,128)}), s32[4,256,1]{1,2,0:T(1,128)S(1)}, u32[]{:S(2)}, u32[]{:S(2)}) %all-to-all-start.1) | async-done | bytes 4128 | tf_op jit(solution)/shard_map/all_to_all | solution.py:56
  52.2 3.5 %all-to-all-start.3 = ((bf16[4,256,512]{2,1,0:T(8,128)(2,1)}), bf16[4,256,512]{2,1,0:T(8,128)(2,1)S(1)}, u32[]{:S(2)}, u32[]{:S(2)}) async-start(bf16[4,256,512]{2,1,0:T(8,128)(2,1)} %bitcast.8), calls=%async_computation.3 | async-start | bytes 2097152 | tf_op jit(solution)/shard_map/all_to_all | solution.py:55
  55.8 12.1 %all-to-all-done.3 = bf16[4,256,512]{2,1,0:T(8,128)(2,1)S(1)} async-done(((bf16[4,256,512]{2,1,0:T(8,128)(2,1)}), bf16[4,256,512]{2,1,0:T(8,128)(2,1)S(1)}, u32[]{:S(2)}, u32[]{:S(2)}) %all-to-all-start.3) | async-done | bytes 1048608 | tf_op jit(solution)/shard_map/all_to_all | solution.py:55
  67.9 24.4 %while.13 = (s32[]{:T(128)}, f32[8016,512]{1,0:T(8,128)}, f32[8016]{0:T(1024)S(1)}, s32[2,512]{1,0:T(2,128)S(1)}, bf16[2,512,512]{2,1,0:T(8,128)(2,1)S(1)}, /*index=5*/s32[]{:T(128)}, s32[]{:T(128)}) while((s32[]{:T(128)}, f32[8016,512]{1,0:T(8,128)}, f32[8016]{0:T(1024)S(1)}, s32[2,512]{1,0:T(2,128)S(1)}, ...), condition=%wide.region_4.5_spmd.clone, body=%wide.region_2.4_spmd.clone.sunk | while | flops 4227325952 | bytes 33494372 | solution.py:82
  67.9 1.8 %fusion.18 = f32[8016]{0:T(1024)S(1)} fusion(s32[512]{0:T(512)S(1)} %bitcast.28), kind=kLoop, calls=%fused_computation.4.clone.1 | loop fusion | flops 12304560 | bytes 34112 | tf_op jit(solution)/shard_map/while/body/eval_jaxpr/reduce_sum | solution.py:75
  69.7 8.7 %select_add_fusion.4 = f32[8016,512]{1,0:T(8,128)} fusion(f32[8016,512]{1,0:T(8,128)} %get-tuple-element.106, s32[512]{0:T(512)S(1)} %bitcast.29, pred[]{:T(512)S(6)} %compare.4, bf16[2,512,512]{2,1,0:T(8,128)(2,1)S(1)} %get-tuple-element.116, s32[]{:T(128)S(6)} %copy.37), kind=kOutput, calls=%fused_computation.5.clone.1 | convolution fusion | flops 4215005184 | bytes 33359876 | tf_op jit(solution)/shard_map/while/body/eval_jaxpr/dot_general | solution.py:69
  78.4 1.8 %fusion.18 = f32[8016]{0:T(1024)S(1)} fusion(s32[512]{0:T(512)S(1)} %bitcast.28), kind=kLoop, calls=%fused_computation.4.clone.1 | loop fusion | flops 12304560 | bytes 34112 | tf_op jit(solution)/shard_map/while/body/eval_jaxpr/reduce_sum | solution.py:75
  80.3 12.0 %select_add_fusion.4 = f32[8016,512]{1,0:T(8,128)} fusion(f32[8016,512]{1,0:T(8,128)} %get-tuple-element.106, s32[512]{0:T(512)S(1)} %bitcast.29, pred[]{:T(512)S(6)} %compare.4, bf16[2,512,512]{2,1,0:T(8,128)(2,1)S(1)} %get-tuple-element.116, s32[]{:T(128)S(6)} %copy.37), kind=kOutput, calls=%fused_computation.5.clone.1 | convolution fusion | flops 4215005184 | bytes 33359876 | tf_op jit(solution)/shard_map/while/body/eval_jaxpr/dot_general | solution.py:69
  92.3 0.6 broadcast_multiply_fusion
  (15 shorter events, 0.1 us)
Async XLA Ops:
  1.9 11.9 %all-to-all-start = ((s32[8,128,1]{1,2,0:T(1,128)}), s32[8,128,1]{1,2,0:T(1,128)S(1)}, u32[]{:S(2)}, u32[]{:S(2)}) async-start(s32[8,128,1]{1,2,0:T(1,128)} %stack.2), calls=%async_computation | async-start | bytes 8192 | tf_op jit(solution)/shard_map/all_to_all | solution.py:45
  13.7 30.1 %all-to-all-start.2 = ((bf16[128,8,512]{2,0,1:T(8,128)(2,1)}), bf16[128,8,512]{2,0,1:T(8,128)(2,1)S(1)}, u32[]{:S(2)}, u32[]{:S(2)}) async-start(bf16[128,8,512]{2,0,1:T(8,128)(2,1)} %copy.30), calls=%async_computation.2 | async-start | bytes 2097152 | tf_op jit(solution)/shard_map/all_to_all | solution.py:43
  43.8 8.4 %all-to-all-start.1 = ((s32[4,256,1]{1,2,0:T(1,128)}), s32[4,256,1]{1,2,0:T(1,128)S(1)}, u32[]{:S(2)}, u32[]{:S(2)}) async-start(s32[4,256,1]{1,2,0:T(1,128)} %copy.26), calls=%async_computation.1 | async-start | bytes 8192 | tf_op jit(solution)/shard_map/all_to_all | solution.py:56
  52.2 15.7 %all-to-all-start.3 = ((bf16[4,256,512]{2,1,0:T(8,128)(2,1)}), bf16[4,256,512]{2,1,0:T(8,128)(2,1)S(1)}, u32[]{:S(2)}, u32[]{:S(2)}) async-start(bf16[4,256,512]{2,1,0:T(8,128)(2,1)} %bitcast.8), calls=%async_computation.3 | async-start | bytes 2097152 | tf_op jit(solution)/shard_map/all_to_all | solution.py:55
